TPU v7x, 32 devices: a whole 2x2x4 slice. The times are simulated.
32 devices in a mesh: fsdp: 4 (over y, x), tenant: 4 (over z), dp: 2 (over core).
Axes of the slice: x: 2, y: 2, z: 4, core: 2. Of those that a mesh axis runs over, the one named last changes fastest.
Arguments:
- tokens: bfloat16 [3072, 5120], P(('fsdp', 'dp'), 'tenant'), may hold values from -6 to 6
- block_tenant_index: int32 [48], P(('fsdp', 'dp')), may hold values from 0 to 7
- ranks: int32 [8], replicated, may hold values from 16 to 64, as said below
- frozen_up_weight: bfloat16 [5120, 14336], P(('fsdp', 'dp'), 'tenant'), may hold values from -0.078125 to 0.078125
- tenant_down_adapters: bfloat16 [8, 64, 5120], P('tenant'), may hold values from -0.078125 to 0.078125
- tenant_up_adapters: bfloat16 [8, 64, 14336], P('tenant'), may hold values from -0.75 to 0.75
- cotangent: bfloat16 [3072, 14336], P(('fsdp', 'dp'), 'tenant'), may hold values from -6 to 6
Outputs:
- hidden_out: bfloat16 [3072, 14336], P(('fsdp', 'dp'), 'tenant')
- grad_tokens: bfloat16 [3072, 5120], P(('fsdp', 'dp'), 'tenant')
- grad_down: float32 [8, 64, 5120], P('dp', None, 'tenant')
- grad_up: float32 [8, 64, 14336], P('dp', None, 'tenant')
Inputs may be any that keep to these rules, and one draw needn't show every extreme that they name: `ranks`: multiples of 16; some tenant has rank 64.
All inputs are finite; a program needn't handle non-finite values.
Results may differ from a plain program's by a relative error of at most 0.0034.
Values may be sent and summed in bfloat16 or wider, within the bound.
A program may use at most 128 MiB of HBM per device.

v0:
```python
import functools
import math

import jax
import jax.numpy as jnp
import numpy as np
from jax import lax
from jax.experimental import pallas as pl
from jax.experimental.pallas import tpu as pltpu
from jax.sharding import PartitionSpec as P

BLOCK = 64
PIECES = 5

alpha_scale = 32.0

BF16 = jnp.bfloat16
F32 = jnp.float32
MESH = pl.DeviceIdType.MESH


def nt(a, b):
    return lax.dot_general(a, b, (((1,), (1,)), ((), ())), preferred_element_type=F32)


def tn(a, b):
    return lax.dot_general(a, b, (((0,), (0,)), ((), ())), preferred_element_type=F32)


def nn(a, b):
    return jnp.dot(a, b, preferred_element_type=F32)


def tile_of(width, most=512):
    return max(t for t in range(128, most + 1, 128) if width % t == 0)


def snake(i, n):
    side = math.isqrt(n)
    if side * side != n:
        return i
    row, col = i // side, i % side
    odd = row % 2
    return row * side + (1 - odd) * col + odd * (side - 1 - col)


def kernel(n, m, tenants_of, ranks, tokens, split, cot, w, dn, up, eye,
           hid_o, gt_o, gr_o,
           wbuf, cotv, tokv, tv, hid, upv, dnv, part, come, gp, dpr, rsr, ags, sums, ada, adg,
           l_sem, ws, wr, os, orr, ds, dr, ts, tr, as_, ar, xs, xr, ss, sr, gs, gr, ps, pr, rs, rr, qs, qr, o_sem, cred):
    f, z, c = lax.axis_index("fsdp"), lax.axis_index("tenant"), lax.axis_index("dp")
    rows, ld = tokens.shape
    lf = cot.shape[1]
    depth = w.shape[0]
    piece = depth // PIECES
    own, rank, _ = dn.shape
    tenants = ranks.shape[0]
    half = n // 2
    share = rank // 2
    quarter = gp.shape[0] // n
    blocks = rows // BLOCK
    tile = tile_of(lf)
    aligned = depth % 128 == 0

    place = snake(f, n)
    right, left = snake((place + 1) % n, n), snake((place + n - 1) % n, n)
    to_right, to_left, partner = (right, z, c), (left, z, c), (f, z, 1 - c)

    def plane(t):
        return (f, t, c)

    def owner(s):
        return snake((place + n - s) % n, n)

    def phys(s):
        return 0 if s in (0, half) else s if s < half else s - 1

    def rcopy(src, dst, send, recv, device):
        return pltpu.make_async_remote_copy(
            src_ref=src, dst_ref=dst, send_sem=send, recv_sem=recv, device_id=device, device_id_type=MESH
        )

    sent = []

    def start(copy, cond=None):
        if cond is None:
            copy.start()
        else:
            pl.when(cond)(copy.start)
        sent.append((cond, copy))

    barrier = pltpu.get_barrier_semaphore()
    for k in range(1, n):
        pl.semaphore_signal(barrier, inc=1, device_id=(snake((place + k) % n, n), z, c), device_id_type=MESH)
    for k in range(1, m):
        pl.semaphore_signal(barrier, inc=1, device_id=plane((z + k) % m), device_id_type=MESH)
    pl.semaphore_signal(barrier, inc=1, device_id=partner, device_id_type=MESH)

    def tok_src(ca):
        return tokens.at[:, ca * depth:(ca + 1) * depth] if aligned else split.at[ca]

    local = [
        pltpu.make_async_copy(w.reshape(PIECES, piece, lf), wbuf.at[0, 0], l_sem.at[0]),
        pltpu.make_async_copy(cot, cotv, l_sem.at[1]),
        pltpu.make_async_copy(tokens, tokv, l_sem.at[2]),
        pltpu.make_async_copy(tok_src(0), tv.at[z, 0], l_sem.at[3]),
        pltpu.make_async_copy(tok_src(1), tv.at[z, 1], l_sem.at[4]),
        pltpu.make_async_copy(
            dn.at[:, :, pl.ds(pl.multiple_of(z * ld, 128), ld)], dnv.at[pl.ds(z * own, own)], l_sem.at[5]),
        pltpu.make_async_copy(
            up.at[:, :, pl.ds(pl.multiple_of(z * lf, 128), lf)], upv.at[pl.ds(z * own, own)], l_sem.at[6]),
    ]
    for copy in local:
        copy.start()
    pl.semaphore_wait(barrier, n + m - 1)

    pieces = w.reshape(PIECES, piece, lf)
    for i in range(PIECES):
        a, b = i, PIECES - 1 - i
        start(rcopy(pieces.at[a], wbuf.at[0, phys(1), a], ws.at[0, 0, a], wr.at[0, 0, a], to_right))
        start(rcopy(pieces.at[b], wbuf.at[0, phys(n - 1), b], ws.at[0, 1, b], wr.at[0, 1, b], to_left))
    start(rcopy(pieces, wbuf.at[1, 0], os.at[0], orr.at[0], partner))

    for ca in range(2):
        start(rcopy(tok_src(ca), tv.at[z, ca], ts.at[0, 0, ca], tr.at[z, ca], plane(z + 1)), z < m - 1)
        start(rcopy(tok_src(ca), tv.at[z, ca], ts.at[0, 1, ca], tr.at[z, ca], plane(z - 1)), z > 0)

    def send_adapters(way, cond):
        step = 1 if way == 0 else -1
        mine = pl.ds(pl.multiple_of(c * share, 16), share)
        for j in range(1, m):
            t = z + step * j
            inside = cond & ((t < m) if way == 0 else (t >= 0))
            for kind, (src, dst, width) in enumerate(((dn, dnv, ld), (up, upv, lf))):
                start(rcopy(
                    src.at[:, mine, pl.ds(pl.multiple_of(t * width, 128), width)],
                    dst.at[pl.ds(z * own, own), mine],
                    as_.at[way, j - 1, kind], ar.at[way, j - 1, kind], plane(t)), inside)

    def hop(s, cc):
        d = owner(s)
        upward = (d > z).astype(jnp.int32)
        t = z + 2 * upward - 1
        last_down = (1 - upward) * (t == d).astype(jnp.int32)
        slot = s + (n - s) * last_down
        return rcopy(part.at[s, cc], come.at[slot, cc], gs.at[s, cc], gr.at[slot, cc], plane(t))

    def product(s, cc, ph):
        d = owner(s)
        block = wbuf[cc, ph].reshape(depth, lf)
        part[s, cc] = nt(cotv[...], block).astype(BF16)
        pl.when(((d > z) & (z == 0)) | ((d < z) & (z == m - 1)))(hop(s, cc).start)

    def combine(s, cc, pos):
        d = owner(s)

        @pl.when(((d > z) & (z == pos)) | ((d < z) & (m - 1 - z == pos)))
        def _():
            rcopy(part.at[s, cc], come.at[s, cc], gs.at[s, cc], gr.at[s, cc], partner).wait_recv()
            part[s, cc] = (part[s, cc].astype(F32) + come[s, cc].astype(F32)).astype(BF16)
            hop(s, cc).start()

    def combine_all(first, count, pos):
        @pl.loop(0, 2 * count)
        def _(i):
            k = i // 2
            s = first + k + (k // (half - 1)) * (1 if first else 0)
            combine(s, i % 2, pos)

    local[0].wait()
    local[1].wait()

    product(0, 0, 0)
    rcopy(pieces, wbuf.at[1, 0], os.at[0], orr.at[0], partner).wait_recv()
    product(0, 1, 0)

    send_adapters(0, z == 0)
    send_adapters(1, z == m - 1)
    for k in range(1, m):
        for way, t, there in ((0, z - k, z - k >= 0), (1, z + k, z + k < m)):
            nxt = z + 1 if way == 0 else z - 1
            more = there & ((nxt < m) if way == 0 else (nxt >= 0))
            for ca in range(2):
                pl.when(there)(rcopy(
                    tv.at[t, ca], tv.at[t, ca], ts.at[0, 0, ca], tr.at[t, ca], partner).wait_recv)
                if k < m - 1:
                    start(rcopy(tv.at[t, ca], tv.at[t, ca], ts.at[k, way, ca], tr.at[t, ca], plane(nxt)), more)
        send_adapters(0, z == k)
        send_adapters(1, m - 1 - z == k)

    for copy in local[2:]:
        copy.wait()

    def feature(s, cc):
        core = c if cc == 0 else 1 - c
        return tv[owner(s), core]

    def forward(spots, body):
        @pl.loop(0, lf // tile)
        def _(j):
            columns = pl.ds(pl.multiple_of(j * tile, tile), tile)
            total = None
            for s, cc in spots:
                block = wbuf[cc, phys(s), :, :, columns].reshape(depth, tile)
                term = nn(feature(s, cc), block)
                total = term if total is None else total + term
            body(columns, total)

    def set_hid(columns, total):
        hid[:, columns] = total

    def add_hid(columns, total):
        hid[:, columns] += total

    forward(((0, 0), (0, 1)), set_hid)
    pl.semaphore_signal(cred.at[0], inc=1, device_id=to_left, device_id_type=MESH)
    pl.semaphore_signal(cred.at[1], inc=1, device_id=to_right, device_id_type=MESH)
    pl.semaphore_signal(cred.at[2], inc=1, device_id=partner, device_id_type=MESH)

    pl.semaphore_wait(cred.at[0], 1)
    pl.semaphore_wait(cred.at[1], 1)

    def arrived(stage, way, i, ph):
        rcopy(wbuf.at[0, ph, i], wbuf.at[0, ph, i], ws.at[stage, way, i], wr.at[stage, way, i], partner).wait_recv()

    def across(s, i):
        start(rcopy(wbuf.at[0, phys(s), i], wbuf.at[1, phys(s), i], ds.at[s, i], dr.at[s, i], partner))

    mid = PIECES // 2
    for stage in range(half - 1):
        last = stage == half - 2
        for i in range(PIECES):
            for way in range(2):
                q = i if way == 0 else PIECES - 1 - i
                s = stage + 1 if way == 0 else n - stage - 1
                arrived(stage, way, q, phys(s))
                on = stage + 2 if way == 0 else n - stage - 2
                if not last or i < mid:
                    start(rcopy(wbuf.at[0, phys(s), q], wbuf.at[0, phys(on), q], ws.at[stage + 1, way, q],
                                wr.at[stage + 1, way, q], to_right if way == 0 else to_left))
                across(s, q)
            if last and i == mid:
                ph = phys(half - 1) * (1 - c) + phys(half + 1) * c
                start(rcopy(wbuf.at[0, ph, mid], wbuf.at[0, 0, mid], ws.at[half - 1, 0, mid], wr.at[half - 1, 0, mid],
                            (right * (1 - c) + left * c, z, c)))
    for pos in range(1, m - 1):
        combine_all(0, 1, pos)

    for j in range(1, m):
        for way, t, there in ((0, z - j, z - j >= 0), (1, z + j, z + j < m)):
            for kind, dst in enumerate((dnv, upv)):
                block = dst.at[pl.ds(t * own, own), pl.ds(pl.multiple_of(c * share, 16), share)]
                pl.when(there)(rcopy(
                    block, block, as_.at[way, j - 1, kind], ar.at[way, j - 1, kind], partner).wait_recv)
                start(rcopy(block, block, xs.at[way, j - 1, kind], xr.at[way, j - 1, kind], partner), there)
    for j in range(1, m):
        for way, t, there in ((0, z - j, z - j >= 0), (1, z + j, z + j < m)):
            for kind, dst in enumerate((dnv, upv)):
                block = dst.at[pl.ds(t * own, own), pl.ds(pl.multiple_of((1 - c) * share, 16), share)]
                pl.when(there)(rcopy(
                    block, block, xs.at[way, j - 1, kind], xr.at[way, j - 1, kind], partner).wait_recv)

    @pl.loop(0, blocks)
    def _(b):
        t = tenants_of[b]
        at = pl.ds(pl.multiple_of(b * BLOCK, BLOCK), BLOCK)
        down_t, up_t = dnv[t], upv[t]
        first = nt(tokv[at, :], jnp.concatenate([down_t, jnp.zeros_like(down_t)], axis=0))
        second = nt(cotv[at, :], jnp.concatenate([jnp.zeros_like(up_t), up_t], axis=0))
        sums[z, at, :] = first + second

    for j in range(1, m):
        t = (z + j) % m
        start(rcopy(sums.at[z], sums.at[z], ss.at[j - 1], sr.at[z], plane(t)))

    for i in range(n - 2):
        s = 1 + i + i // (half - 1)
        for q in range(PIECES):
            rcopy(wbuf.at[1, phys(s), q], wbuf.at[1, phys(s), q], ds.at[s, q], dr.at[s, q], partner).wait_recv()

    @pl.loop(0, 2 * (n - 2))
    def _(i):
        k = i // 2
        product(1 + k + k // (half - 1), i % 2, 1 + k)

    for i in range(n - 2):
        s = 1 + i + i // (half - 1)
        forward(((s, 0), (s, 1)), add_hid)
        for pos in range(1, m - 1):
            if i == min(pos - 1, n - 3):
                combine_all(1, n - 2, pos)

    for j in range(1, m):
        t = (z + j) % m
        rcopy(sums.at[t], sums.at[t], ss.at[j - 1], sr.at[t], partner).wait_recv()

    @pl.loop(0, blocks)
    def _(b):
        t = tenants_of[b]
        r = ranks[t]
        at = pl.ds(pl.multiple_of(b * BLOCK, BLOCK), BLOCK)
        total = sums[0, at, :]
        for k in range(1, m):
            total = total + sums[k, at, :]
        lane = lax.broadcasted_iota(jnp.int32, total.shape, 1)
        slot = jnp.where(lane >= rank, lane - rank, lane)
        width = jnp.full(total.shape, r, jnp.int32).astype(F32)
        gain = jnp.where(slot < r, alpha_scale / width, 0.0)
        scaled = (total * gain).astype(BF16)
        column = lax.broadcasted_iota(jnp.int32, (BLOCK, tenants * rank), 1)
        mine = (column >= t * rank) & (column < (t + 1) * rank)
        ada[at, :] = jnp.where(mine, nn(scaled, eye[0]), 0.0).astype(BF16)
        adg[at, :] = jnp.where(mine, nn(scaled, eye[1]), 0.0).astype(BF16)

    tall = gp.shape[0]

    def grads(core, other):
        lanes = pl.ds(pl.multiple_of(core * tall, 128), tall)

        @pl.loop(0, lf // tile)
        def _(j):
            columns = pl.ds(pl.multiple_of(j * tile, tile), tile)
            term = tn(ada[:, lanes], cotv[:, columns])
            if other is not None:
                term = term + other[:, columns].astype(F32)
            gp[:, columns] = term.astype(BF16)

        term = tn(adg[:, lanes], tokv[...])
        if other is not None:
            term = term + other[:, lf:].astype(F32)
        gp[:, lf:] = term.astype(BF16)

    grads(1 - c, None)
    swap = rcopy(gp, dpr, ps.at[0], pr.at[0], partner)
    swap.start()
    swap.wait()
    grads(c, dpr)
    for k in range(1, n):
        peer = snake((place + k) % n, n)
        start(rcopy(gp.at[pl.ds(pl.multiple_of(peer * quarter, 16), quarter)], rsr.at[k - 1], rs.at[k - 1],
                    rr.at[k - 1], (peer, z, c)))

    pl.semaphore_wait(cred.at[2], 1)
    for i in range(mid):
        for way in range(2):
            q = i if way == 0 else PIECES - 1 - i
            arrived(half - 1, way, q, 0)
            across(half, q)
    arrived(half - 1, 0, mid, 0)
    across(half, mid)
    product(half, 0, 0)
    for q in range(PIECES):
        rcopy(wbuf.at[1, 0, q], wbuf.at[1, 0, q], ds.at[half, q], dr.at[half, q], partner).wait_recv()
    product(half, 1, 0)

    for k in range(1, n):
        rcopy(rsr.at[k - 1], rsr.at[k - 1], rs.at[k - 1], rr.at[k - 1], partner).wait_recv()
    total = gp[pl.ds(pl.multiple_of(f * quarter, 16), quarter), :].astype(F32)
    for k in range(1, n):
        total = total + rsr[k - 1].astype(F32)
    ags[...] = total.astype(BF16)
    for k in range(1, n):
        start(rcopy(ags, gr_o.at[f], qs.at[k - 1], qr.at[k - 1], (snake((place + k) % n, n), z, c)))
    keep = pltpu.make_async_copy(ags, gr_o.at[f], o_sem.at[0])
    keep.start()

    for pos in range(1, m - 1):
        for cc in range(2):
            combine(half, cc, pos)

    up_flat = tenants * rank

    def finish(columns, total):
        total = total + nn(ada[...], upv[:, :, columns].reshape(up_flat, tile))
        cotv[:, columns] = (hid[:, columns] + total).astype(BF16)

    forward(((half, 0), (half, 1)), finish)
    hidden = pltpu.make_async_copy(cotv, hid_o, o_sem.at[1])
    hidden.start()

    s_z = (place + n - snake(z, n)) % n
    for slots, cond in (((n,), z == 0), ((s_z,), z == m - 1), ((s_z, n), (z > 0) & (z < m - 1))):
        @pl.when(cond)
        def _():
            for slot in slots:
                for cc in range(2):
                    rcopy(come.at[slot, cc], come.at[slot, cc], gs.at[0, cc], gr.at[slot, cc], partner).wait_recv()
            term = nn(adg[...], dnv[...].reshape(up_flat, ld))
            for ca in range(2):
                cc = ca + c - 2 * ca * c
                total = term[:, ca * depth:(ca + 1) * depth] + part[s_z, cc].astype(F32)
                for slot in slots:
                    total = total + come[slot, cc].astype(F32)
                tokv[:, ca * depth:(ca + 1) * depth] = total.astype(BF16)

    back = pltpu.make_async_copy(tokv, gt_o, o_sem.at[2])
    back.start()

    for k in range(1, n):
        peer = snake((place + n - k) % n, n)
        rcopy(gr_o.at[peer], gr_o.at[peer], qs.at[k - 1], qr.at[k - 1], partner).wait_recv()
    for cond, copy in sent:
        if cond is None:
            copy.wait_send()
        else:
            pl.when(cond)(copy.wait_send)
    for s in range(n):
        for cc in range(2):
            pl.when(owner(s) != z)(hop(s, cc).wait_send)
    keep.wait()
    hidden.wait()
    back.wait()


def make_shards(mesh):
    n, m, dp_n = mesh.shape["fsdp"], mesh.shape["tenant"], mesh.shape["dp"]
    assert dp_n == 2 and n == m and n % 2 == 0 and n >= 4

    def shards(tokens, block_tenant_index, ranks, frozen_up_weight, tenant_down_adapters,
               tenant_up_adapters, cotangent):
        rows, ld = tokens.shape
        lf = cotangent.shape[1]
        tenants = ranks.shape[0]
        rank = tenant_down_adapters.shape[1]
        depth = frozen_up_weight.shape[0]
        piece = depth // PIECES
        tall = tenants * rank // dp_n
        quarter = tall // n
        half = n // 2
        split = tokens
        if depth % 128:
            split = tokens.reshape(rows, ld // depth, depth).transpose(1, 0, 2)
        eye = np.zeros((2, 2 * rank, tenants * rank), np.float32)
        for t in range(tenants):
            for k in range(2):
                eye[k, k * rank:(k + 1) * rank, t * rank:(t + 1) * rank] = np.eye(rank)

        any_space = pl.BlockSpec(memory_space=pl.ANY)
        dma = pltpu.SemaphoreType.DMA
        hidden, back, grads = pl.pallas_call(
            functools.partial(kernel, n, m),
            out_shape=(
                jax.ShapeDtypeStruct((rows, lf), BF16),
                jax.ShapeDtypeStruct((rows, ld), BF16),
                jax.ShapeDtypeStruct((n, quarter, lf + ld), BF16),
            ),
            in_specs=[pl.BlockSpec(memory_space=pltpu.SMEM)] * 2 + [any_space] * 6
            + [pl.BlockSpec(memory_space=pltpu.VMEM)],
            out_specs=(any_space,) * 3,
            scratch_shapes=[
                pltpu.VMEM((2, n - 1, PIECES, piece, lf), BF16),
                pltpu.VMEM((rows, lf), BF16),
                pltpu.VMEM((rows, ld), BF16),
                pltpu.VMEM((m, 2, rows, depth), BF16),
                pltpu.VMEM((rows, lf), F32),
                pltpu.VMEM((tenants, rank, lf), BF16),
                pltpu.VMEM((tenants, rank, ld), BF16),
                pltpu.VMEM((n, 2, rows, depth), BF16),
                pltpu.VMEM((n + 1, 2, rows, depth), BF16),
                pltpu.VMEM((tall, lf + ld), BF16),
                pltpu.VMEM((tall, lf + ld), BF16),
                pltpu.VMEM((n - 1, quarter, lf + ld), BF16),
                pltpu.VMEM((quarter, lf + ld), BF16),
                pltpu.VMEM((m, rows, 2 * rank), F32),
                pltpu.VMEM((rows, tenants * rank), BF16),
                pltpu.VMEM((rows, tenants * rank), BF16),
                dma((7,)),
                dma((half, 2, PIECES)), dma((half, 2, PIECES)),
                dma((1,)), dma((1,)),
                dma((n, PIECES)), dma((n, PIECES)),
                dma((m - 1, 2, 2)), dma((m, 2)),
                dma((2, m - 1, 2)), dma((2, m - 1, 2)),
                dma((2, m - 1, 2)), dma((2, m - 1, 2)),
                dma((m - 1,)), dma((m,)),
                dma((n, 2)), dma((n + 1, 2)),
                dma((1,)), dma((1,)),
                dma((n - 1,)), dma((n - 1,)),
                dma((n - 1,)), dma((n - 1,)),
                dma((3,)),
                pltpu.SemaphoreType.REGULAR((3,)),
            ],
            compiler_params=pltpu.CompilerParams(
                collective_id=0, has_side_effects=True, vmem_limit_bytes=67043328
            ),
        )(block_tenant_index, ranks, tokens, split, cotangent, frozen_up_weight,
          tenant_down_adapters, tenant_up_adapters, jnp.asarray(eye, BF16))
        grads = grads.reshape(tall, lf + ld).astype(F32)
        grad_up = grads[:, :lf].reshape(tenants // dp_n, rank, lf)
        grad_down = grads[:, lf:].reshape(tenants // dp_n, rank, ld)
        return (hidden, back, grad_down, grad_up)

    return shards


def solution(mesh):
    return jax.shard_map(
        make_shards(mesh),
        mesh=mesh,
        in_specs=(
            P(("fsdp", "dp"), "tenant"),
            P(("fsdp", "dp")),
            P(),
            P(("fsdp", "dp"), "tenant"),
            P("tenant", None, None),
            P("tenant", None, None),
            P(("fsdp", "dp"), "tenant"),
        ),
        out_specs=(
            P(("fsdp", "dp"), "tenant"),
            P(("fsdp", "dp"), "tenant"),
            P("dp", None, "tenant"),
            P("dp", None, "tenant"),
        ),
        check_vma=False,
    )
```

profile of v0, /device:TPU:7, one launch (start us, length us, event | category | flops | bytes accessed | tf_op | source)
XLA Modules:
  0.0 263.4 jit_solution(14920712468025338367)
XLA Ops:
  0.6 254.1 %shard_map.111 = (bf16[384,3584]{1,0:T(8,128)(2,1)}, bf16[384,1280]{1,0:T(8,128)(2,1)}, bf16[4,64,4864]{2,1,0:T(8,128)(2,1)}) custom-call(s32[6]{0:T(128)} %tenants_of.1, s32[8]{0:T(128)} %ranks.1, bf16[384,1280]{1,0:T(8,128)(2,1)} %split.1, bf16[384,1280]{1,0:T(8,128)(2,1)} %split.1, bf16[384,3584]{1,0:T(8,128)(2,1)} %cot.1, bf16[640,3584]{1,0:T(8,128)(2,1)} %w.1, ...), custom_call_target="tpu_custom_call" | custom-call | tf_op jit(solution)/shard_map/pallas_call | solution.py:440
  254.8 2.0 bitcast_convert_fusion
  256.8 1.1 slice.8
  257.9 0.0 copy-start
  257.9 2.3 slice.9
  260.3 0.3 copy-done
  260.5 0.0 copy-start.1
  260.5 1.5 copy.14
  262.1 0.4 copy-done.1
  262.4 0.9 copy.15
Async XLA Ops:
  257.9 2.6 copy-start
  260.5 1.9 copy-start.1
where the time goes:
time: 265 us; the launch traced here: 263 us
  Pallas kernels  254 us (96%)
  local copies, waits for them, and re-layouts  6.55 us (2%)
    pallas_call x1, Pallas kernels, shards(): pl.pallas_call(functools.partial(kernel, n, m), out_shape=(jax.ShapeDtype...  254 us

commit v1 on v0

v1 whole, which is shorter than its diff:
```python
import functools
import math

import jax
import jax.numpy as jnp
import numpy as np
from jax import lax
from jax.experimental import pallas as pl
from jax.experimental.pallas import tpu as pltpu
from jax.sharding import PartitionSpec as P

BLOCK = 64
PIECES = 5

alpha_scale = 32.0

BF16 = jnp.bfloat16
F32 = jnp.float32
MESH = pl.DeviceIdType.MESH


def nt(a, b):
    return lax.dot_general(a, b, (((1,), (1,)), ((), ())), preferred_element_type=F32)


def tn(a, b):
    return lax.dot_general(a, b, (((0,), (0,)), ((), ())), preferred_element_type=F32)


def nn(a, b):
    return jnp.dot(a, b, preferred_element_type=F32)


def tile_of(width, most=512):
    return max(t for t in range(128, most + 1, 128) if width % t == 0)


def snake(i, n):
    side = math.isqrt(n)
    if side * side != n:
        return i
    row, col = i // side, i % side
    odd = row % 2
    return row * side + (1 - odd) * col + odd * (side - 1 - col)


def kernel(n, m, tenants_of, ranks, tokens, split, cot, w, dn, up, eye,
           hid_o, gt_o, gu_o, gd_o, pair_o,
           wbuf, cotv, tokv, tv, hid, upv, dnv, part, come, gp, dpr, rsr, ags, sums, ada, adg,
           l_sem, ws, wr, os, orr, ds, dr, ts, tr, as_, ar, xs, xr, ss, sr, gs, gr, ps, pr, rs, rr, qs, qr, o_sem, cred):
    f, z, c = lax.axis_index("fsdp"), lax.axis_index("tenant"), lax.axis_index("dp")
    rows, ld = tokens.shape
    lf = cot.shape[1]
    depth = w.shape[0]
    piece = depth // PIECES
    own, rank, _ = dn.shape
    tenants = ranks.shape[0]
    half = n // 2
    share = rank // 2
    quarter = gp.shape[0] // n
    blocks = rows // BLOCK
    tile = tile_of(lf)
    aligned = depth % 128 == 0

    place = snake(f, n)
    right, left = snake((place + 1) % n, n), snake((place + n - 1) % n, n)
    to_right, to_left, partner = (right, z, c), (left, z, c), (f, z, 1 - c)

    def plane(t):
        return (f, t, c)

    def owner(s):
        return snake((place + n - s) % n, n)

    def phys(s):
        return 0 if s in (0, half) else s if s < half else s - 1

    def rcopy(src, dst, send, recv, device):
        return pltpu.make_async_remote_copy(
            src_ref=src, dst_ref=dst, send_sem=send, recv_sem=recv, device_id=device, device_id_type=MESH
        )

    sent = []

    def start(copy, cond=None):
        if cond is None:
            copy.start()
        else:
            pl.when(cond)(copy.start)
        sent.append((cond, copy))

    barrier = pltpu.get_barrier_semaphore()
    for k in range(1, n):
        pl.semaphore_signal(barrier, inc=1, device_id=(snake((place + k) % n, n), z, c), device_id_type=MESH)
    for k in range(1, m):
        pl.semaphore_signal(barrier, inc=1, device_id=plane((z + k) % m), device_id_type=MESH)
    pl.semaphore_signal(barrier, inc=1, device_id=partner, device_id_type=MESH)

    def tok_src(ca):
        return tokens.at[:, ca * depth:(ca + 1) * depth] if aligned else split.at[ca]

    local = [
        pltpu.make_async_copy(w.reshape(PIECES, piece, lf), wbuf.at[0, 0], l_sem.at[0]),
        pltpu.make_async_copy(cot, cotv, l_sem.at[1]),
        pltpu.make_async_copy(tokens, tokv, l_sem.at[2]),
        pltpu.make_async_copy(tok_src(0), tv.at[z, 0], l_sem.at[3]),
        pltpu.make_async_copy(tok_src(1), tv.at[z, 1], l_sem.at[4]),
        pltpu.make_async_copy(
            dn.at[:, :, pl.ds(pl.multiple_of(z * ld, 128), ld)], dnv.at[pl.ds(z * own, own)], l_sem.at[5]),
        pltpu.make_async_copy(
            up.at[:, :, pl.ds(pl.multiple_of(z * lf, 128), lf)], upv.at[pl.ds(z * own, own)], l_sem.at[6]),
    ]
    for copy in local:
        copy.start()
    pl.semaphore_wait(barrier, n + m - 1)

    pieces = w.reshape(PIECES, piece, lf)
    for i in range(PIECES):
        a, b = i, PIECES - 1 - i
        start(rcopy(pieces.at[a], wbuf.at[0, phys(1), a], ws.at[0, 0, a], wr.at[0, 0, a], to_right))
        start(rcopy(pieces.at[b], wbuf.at[0, phys(n - 1), b], ws.at[0, 1, b], wr.at[0, 1, b], to_left))
    start(rcopy(pieces, wbuf.at[1, 0], os.at[0], orr.at[0], partner))
    start(rcopy(pieces, pair_o, os.at[1], orr.at[1], partner))

    sides = [(way, j, z - j if way == 0 else z + j, (z - j >= 0) if way == 0 else (z + j < m))
             for j in range(1, m) for way in range(2)]
    mine, others = [pl.ds(pl.multiple_of(x * share, 16), share) for x in (c, 1 - c)]
    for j in range(1, m):
        for way, t, there in ((0, z + j, z + j < m), (1, z - j, z - j >= 0)):
            for kind, (src, dst, width) in enumerate(((dn, dnv, ld), (up, upv, lf))):
                start(rcopy(
                    src.at[:, mine, pl.ds(pl.multiple_of(t * width, 128), width)],
                    dst.at[pl.ds(z * own, own), mine],
                    as_.at[way, j - 1, kind], ar.at[way, j - 1, kind], plane(t)), there)
    for ca in range(2):
        start(rcopy(tok_src(ca), tv.at[z, ca], ts.at[0, 0, ca], tr.at[z, ca], plane(z + 1)), z < m - 1)
        start(rcopy(tok_src(ca), tv.at[z, ca], ts.at[0, 1, ca], tr.at[z, ca], plane(z - 1)), z > 0)

    def rows_of(h):
        return pl.ds(pl.multiple_of(h * (rows // 2), 16), rows // 2)

    def hop(s, cc, h):
        d = owner(s)
        upward = (d > z).astype(jnp.int32)
        t = z + 2 * upward - 1
        last_down = (1 - upward) * (t == d).astype(jnp.int32)
        slot = s + (n - s) * last_down
        return rcopy(part.at[s, cc, rows_of(h)], come.at[slot, cc, rows_of(h)], gs.at[s, cc, h], gr.at[slot, cc, h],
                     plane(t))

    def product(s, cc, ph):
        block = wbuf[cc, ph].reshape(depth, lf)
        part[s, cc] = nt(cotv[...], block).astype(BF16)

    def first_hop(s, cc):
        d = owner(s)

        @pl.when(((d > z) & (z == 0)) | ((d < z) & (z == m - 1)))
        def _():
            for h in range(2):
                hop(s, cc, h).start()

    def combine(s, cc, h, pos):
        d = owner(s)
        at = rows_of(h)

        @pl.when(((d > z) & (z == pos)) | ((d < z) & (m - 1 - z == pos)))
        def _():
            rcopy(part.at[s, cc, at], come.at[s, cc, at], gs.at[s, cc, h], gr.at[s, cc, h], partner).wait_recv()
            part[s, cc, at] = (part[s, cc, at].astype(F32) + come[s, cc, at].astype(F32)).astype(BF16)
            hop(s, cc, h).start()

    def combine_all(first, count, pos):
        @pl.loop(0, 4 * count)
        def _(i):
            k = i // 4
            s = first + k + (k // (half - 1)) * (1 if first else 0)
            combine(s, (i // 2) % 2, i % 2, pos)

    local[0].wait()
    local[1].wait()
    product(0, 0, 0)
    rcopy(pieces, wbuf.at[1, 0], os.at[0], orr.at[0], partner).wait_recv()
    product(0, 1, 0)

    pl.semaphore_signal(cred.at[0], inc=1, device_id=to_left, device_id_type=MESH)
    pl.semaphore_signal(cred.at[1], inc=1, device_id=to_right, device_id_type=MESH)
    pl.semaphore_signal(cred.at[2], inc=1, device_id=partner, device_id_type=MESH)
    for copy in local[2:]:
        copy.wait()
    for k in range(3):
        pl.semaphore_wait(cred.at[k], 1)

    mid = PIECES // 2

    def arrived(stage, way, i, ph):
        rcopy(wbuf.at[0, ph, i], wbuf.at[0, ph, i], ws.at[stage, way, i], wr.at[stage, way, i], partner).wait_recv()

    def across(s, i):
        start(rcopy(wbuf.at[0, phys(s), i], wbuf.at[1, phys(s), i], ds.at[s, i], dr.at[s, i], partner))

    def relay(stage, i):
        last = stage == half - 2
        for way in range(2):
            q = i if way == 0 else PIECES - 1 - i
            s = stage + 1 if way == 0 else n - stage - 1
            arrived(stage, way, q, phys(s))
            on = stage + 2 if way == 0 else n - stage - 2
            if not last or i < mid:
                start(rcopy(wbuf.at[0, phys(s), q], wbuf.at[0, phys(on), q], ws.at[stage + 1, way, q],
                            wr.at[stage + 1, way, q], to_right if way == 0 else to_left))
            across(s, q)
        if last and i == mid:
            ph = phys(half - 1) * (1 - c) + phys(half + 1) * c
            start(rcopy(wbuf.at[0, ph, mid], wbuf.at[0, 0, mid], ws.at[half - 1, 0, mid], wr.at[half - 1, 0, mid],
                        (right * (1 - c) + left * c, z, c)))

    for stage in range(half - 2):
        for i in range(PIECES):
            relay(stage, i)
    for i in range(mid):
        relay(half - 2, i)

    for way, j, t, there in sides:
        for kind, dst in enumerate((dnv, upv)):
            block = dst.at[pl.ds(t * own, own), mine]
            pl.when(there)(rcopy(
                block, block, as_.at[way, j - 1, kind], ar.at[way, j - 1, kind], partner).wait_recv)
            start(rcopy(block, block, xs.at[way, j - 1, kind], xr.at[way, j - 1, kind], partner), there)
    for way, j, t, there in sides:
        for kind, dst in enumerate((dnv, upv)):
            block = dst.at[pl.ds(t * own, own), others]
            pl.when(there)(rcopy(
                block, block, xs.at[way, j - 1, kind], xr.at[way, j - 1, kind], partner).wait_recv)

    @pl.loop(0, blocks)
    def _(b):
        t = tenants_of[b]
        at = pl.ds(pl.multiple_of(b * BLOCK, BLOCK), BLOCK)
        down_t, up_t = dnv[t], upv[t]
        first = nt(tokv[at, :], jnp.concatenate([down_t, jnp.zeros_like(down_t)], axis=0))
        second = nt(cotv[at, :], jnp.concatenate([jnp.zeros_like(up_t), up_t], axis=0))
        sums[z, at, :] = first + second

    for j in range(1, m):
        t = (z + j) % m
        start(rcopy(sums.at[z], sums.at[z], ss.at[j - 1], sr.at[z], plane(t)))
    first_hop(0, 0)
    first_hop(0, 1)

    def pass_tokens(k):
        for way, t, there in ((0, z - k, z - k >= 0), (1, z + k, z + k < m)):
            nxt = z + 1 if way == 0 else z - 1
            more = there & ((nxt < m) if way == 0 else (nxt >= 0))
            for ca in range(2):
                pl.when(there)(rcopy(
                    tv.at[t, ca], tv.at[t, ca], ts.at[0, 0, ca], tr.at[t, ca], partner).wait_recv)
                if k < m - 1:
                    start(rcopy(tv.at[t, ca], tv.at[t, ca], ts.at[k, way, ca], tr.at[t, ca], plane(nxt)), more)

    relay(half - 2, mid)
    pass_tokens(1)
    for i in range(mid + 1, PIECES):
        relay(half - 2, i)

    for j in range(1, m):
        t = (z + j) % m
        rcopy(sums.at[t], sums.at[t], ss.at[j - 1], sr.at[t], partner).wait_recv()

    @pl.loop(0, blocks)
    def _(b):
        t = tenants_of[b]
        r = ranks[t]
        at = pl.ds(pl.multiple_of(b * BLOCK, BLOCK), BLOCK)
        total = sums[0, at, :]
        for k in range(1, m):
            total = total + sums[k, at, :]
        lane = lax.broadcasted_iota(jnp.int32, total.shape, 1)
        slot = jnp.where(lane >= rank, lane - rank, lane)
        width = jnp.full(total.shape, r, jnp.int32).astype(F32)
        gain = jnp.where(slot < r, alpha_scale / width, 0.0)
        scaled = (total * gain).astype(BF16)
        column = lax.broadcasted_iota(jnp.int32, (BLOCK, tenants * rank), 1)
        chosen = (column >= t * rank) & (column < (t + 1) * rank)
        ada[at, :] = jnp.where(chosen, nn(scaled, eye[0]), 0.0).astype(BF16)
        adg[at, :] = jnp.where(chosen, nn(scaled, eye[1]), 0.0).astype(BF16)

    tall = gp.shape[0]

    def grads(core, other):
        lanes = pl.ds(pl.multiple_of(core * tall, 128), tall)

        @pl.loop(0, lf // tile)
        def _(j):
            columns = pl.ds(pl.multiple_of(j * tile, tile), tile)
            term = tn(ada[:, lanes], cotv[:, columns])
            if other is not None:
                term = term + other[:, columns].astype(F32)
            gp[:, columns] = term.astype(BF16)

        term = tn(adg[:, lanes], tokv[...])
        if other is not None:
            term = term + other[:, lf:].astype(F32)
        gp[:, lf:] = term.astype(BF16)

    grads(1 - c, None)
    swap = rcopy(gp, dpr, ps.at[0], pr.at[0], partner)
    swap.start()
    combine_all(0, 1, 1)
    swap.wait()
    grads(c, dpr)
    for k in range(2, m - 1):
        pass_tokens(k)

    for i in range(n - 2):
        s = 1 + i + i // (half - 1)
        for q in range(PIECES):
            rcopy(wbuf.at[1, phys(s), q], wbuf.at[1, phys(s), q], ds.at[s, q], dr.at[s, q], partner).wait_recv()

    @pl.loop(0, 2 * (n - 2))
    def _(i):
        k = i // 2
        product(1 + k + k // (half - 1), i % 2, 1 + k)
        first_hop(1 + k + k // (half - 1), i % 2)

    for pos in range(2, m - 1):
        combine_all(0, 1, pos)

    pass_tokens(m - 1)

    def far(i):
        for way in range(2):
            q = i if way == 0 else PIECES - 1 - i
            arrived(half - 1, way, q, 0)
            across(half, q)

    far(0)

    def forward(spots, body):
        spots = [(s, cc, ph if isinstance(ph, tuple) else (cc, ph)) for s, cc, ph in spots]

        @pl.loop(0, lf // tile)
        def _(j):
            columns = pl.ds(pl.multiple_of(j * tile, tile), tile)
            total = None
            for s, cc, ph in spots:
                block = wbuf[ph[0], ph[1], :, :, columns].reshape(depth, tile)
                term = nn(tv[owner(s), c if cc == 0 else 1 - c], block)
                total = term if total is None else total + term
            body(columns, total)

    def set_hid(columns, total):
        hid[:, columns] = total

    def add_hid(columns, total):
        hid[:, columns] += total

    for i in range(n - 2):
        s = 1 + i + i // (half - 1)
        forward(((s, 0, phys(s)), (s, 1, phys(s))), add_hid if i else set_hid)

    for k in range(1, n):
        peer = snake((place + k) % n, n)
        start(rcopy(gp.at[pl.ds(pl.multiple_of(peer * quarter, 16), quarter)], rsr.at[k - 1], rs.at[k - 1],
                    rr.at[k - 1], (peer, z, c)))

    rcopy(pieces, pair_o, os.at[1], orr.at[1], partner).wait_recv()
    again = [pltpu.make_async_copy(pieces, wbuf.at[1, 1], l_sem.at[0]),
             pltpu.make_async_copy(pair_o, wbuf.at[1, 2], l_sem.at[1])]
    for copy in again:
        copy.start()
    for i in range(1, mid):
        far(i)
    combine_all(1, n - 2, 1)
    for copy in again:
        copy.wait()
    forward(((0, 0, (1, 1)), (0, 1, (1, 2))), add_hid)

    arrived(half - 1, 0, mid, 0)
    across(half, mid)
    product(half, 0, 0)
    first_hop(half, 0)
    for q in range(PIECES):
        rcopy(wbuf.at[1, 0, q], wbuf.at[1, 0, q], ds.at[half, q], dr.at[half, q], partner).wait_recv()
    product(half, 1, 0)
    first_hop(half, 1)
    for pos in range(2, m - 1):
        combine_all(1, n - 2, pos)

    up_flat = tenants * rank

    def finish(columns, total):
        total = total + nn(ada[...], upv[:, :, columns].reshape(up_flat, tile))
        cotv[:, columns] = (hid[:, columns] + total).astype(BF16)

    forward(((half, 0, 0), (half, 1, 0)), finish)
    hidden = pltpu.make_async_copy(cotv, hid_o, o_sem.at[2])
    hidden.start()
    for h in range(2):
        combine(half, 0, h, 1)

    for k in range(1, n):
        rcopy(rsr.at[k - 1], rsr.at[k - 1], rs.at[k - 1], rr.at[k - 1], partner).wait_recv()
    total = gp[pl.ds(pl.multiple_of(f * quarter, 16), quarter), :].astype(F32)
    for k in range(1, n):
        total = total + rsr[k - 1].astype(F32)
    ags[...] = total.astype(BF16)
    pair = ((ags.at[:, :lf], gu_o), (ags.at[:, lf:], gd_o))
    keep = [pltpu.make_async_copy(src, dst.at[f], o_sem.at[i]) for i, (src, dst) in enumerate(pair)]
    for k in range(1, n):
        for i, (src, dst) in enumerate(pair):
            start(rcopy(src, dst.at[f], qs.at[k - 1, i], qr.at[k - 1, i], (snake((place + k) % n, n), z, c)))
    for copy in keep:
        copy.start()
    for h in range(2):
        combine(half, 1, h, 1)
    for pos in range(2, m - 1):
        for cc in range(2):
            for h in range(2):
                combine(half, cc, h, pos)

    s_z = (place + n - snake(z, n)) % n
    for slots, cond in (((n,), z == 0), ((s_z,), z == m - 1), ((s_z, n), (z > 0) & (z < m - 1))):
        @pl.when(cond)
        def _():
            for slot in slots:
                for cc in range(2):
                    for h in range(2):
                        at = rows_of(h)
                        rcopy(come.at[slot, cc, at], come.at[slot, cc, at], gs.at[0, cc, h], gr.at[slot, cc, h],
                              partner).wait_recv()
            term = nn(adg[...], dnv[...].reshape(up_flat, ld))
            for ca in range(2):
                cc = ca + c - 2 * ca * c
                total = term[:, ca * depth:(ca + 1) * depth] + part[s_z, cc].astype(F32)
                for slot in slots:
                    total = total + come[slot, cc].astype(F32)
                tokv[:, ca * depth:(ca + 1) * depth] = total.astype(BF16)

    back = pltpu.make_async_copy(tokv, gt_o, o_sem.at[3])
    back.start()

    for k in range(1, n):
        peer = snake((place + n - k) % n, n)
        for i, (_, dst) in enumerate(pair):
            rcopy(dst.at[peer], dst.at[peer], qs.at[k - 1, i], qr.at[k - 1, i], partner).wait_recv()
    for cond, copy in sent:
        if cond is None:
            copy.wait_send()
        else:
            pl.when(cond)(copy.wait_send)
    for s in range(n):
        for cc in range(2):
            for h in range(2):
                pl.when(owner(s) != z)(hop(s, cc, h).wait_send)
    for copy in keep:
        copy.wait()
    hidden.wait()
    back.wait()


def make_shards(mesh):
    n, m, dp_n = mesh.shape["fsdp"], mesh.shape["tenant"], mesh.shape["dp"]
    assert dp_n == 2 and n == m and n % 2 == 0 and n >= 4

    def shards(tokens, block_tenant_index, ranks, frozen_up_weight, tenant_down_adapters,
               tenant_up_adapters, cotangent):
        rows, ld = tokens.shape
        lf = cotangent.shape[1]
        tenants = ranks.shape[0]
        rank = tenant_down_adapters.shape[1]
        depth = frozen_up_weight.shape[0]
        piece = depth // PIECES
        tall = tenants * rank // dp_n
        quarter = tall // n
        half = n // 2
        split = tokens
        if depth % 128:
            split = tokens.reshape(rows, ld // depth, depth).transpose(1, 0, 2)
        eye = np.zeros((2, 2 * rank, tenants * rank), np.float32)
        for t in range(tenants):
            for k in range(2):
                eye[k, k * rank:(k + 1) * rank, t * rank:(t + 1) * rank] = np.eye(rank)

        any_space = pl.BlockSpec(memory_space=pl.ANY)
        dma = pltpu.SemaphoreType.DMA
        hidden, back, grad_up, grad_down, _ = pl.pallas_call(
            functools.partial(kernel, n, m),
            out_shape=(
                jax.ShapeDtypeStruct((rows, lf), BF16),
                jax.ShapeDtypeStruct((rows, ld), BF16),
                jax.ShapeDtypeStruct((n, quarter, lf), BF16),
                jax.ShapeDtypeStruct((n, quarter, ld), BF16),
                jax.ShapeDtypeStruct((PIECES, piece, lf), BF16),
            ),
            in_specs=[pl.BlockSpec(memory_space=pltpu.SMEM)] * 2 + [any_space] * 6
            + [pl.BlockSpec(memory_space=pltpu.VMEM)],
            out_specs=(any_space,) * 5,
            scratch_shapes=[
                pltpu.VMEM((2, n - 1, PIECES, piece, lf), BF16),
                pltpu.VMEM((rows, lf), BF16),
                pltpu.VMEM((rows, ld), BF16),
                pltpu.VMEM((m, 2, rows, depth), BF16),
                pltpu.VMEM((rows, lf), F32),
                pltpu.VMEM((tenants, rank, lf), BF16),
                pltpu.VMEM((tenants, rank, ld), BF16),
                pltpu.VMEM((n, 2, rows, depth), BF16),
                pltpu.VMEM((n + 1, 2, rows, depth), BF16),
                pltpu.VMEM((tall, lf + ld), BF16),
                pltpu.VMEM((tall, lf + ld), BF16),
                pltpu.VMEM((n - 1, quarter, lf + ld), BF16),
                pltpu.VMEM((quarter, lf + ld), BF16),
                pltpu.VMEM((m, rows, 2 * rank), F32),
                pltpu.VMEM((rows, tenants * rank), BF16),
                pltpu.VMEM((rows, tenants * rank), BF16),
                dma((7,)),
                dma((half, 2, PIECES)), dma((half, 2, PIECES)),
                dma((2,)), dma((2,)),
                dma((n, PIECES)), dma((n, PIECES)),
                dma((m - 1, 2, 2)), dma((m, 2)),
                dma((2, m - 1, 2)), dma((2, m - 1, 2)),
                dma((2, m - 1, 2)), dma((2, m - 1, 2)),
                dma((m - 1,)), dma((m,)),
                dma((n, 2, 2)), dma((n + 1, 2, 2)),
                dma((1,)), dma((1,)),
                dma((n - 1,)), dma((n - 1,)),
                dma((n - 1, 2)), dma((n - 1, 2)),
                dma((4,)),
                pltpu.SemaphoreType.REGULAR((3,)),
            ],
            compiler_params=pltpu.CompilerParams(
                collective_id=0, has_side_effects=True, vmem_limit_bytes=67043328
            ),
        )(block_tenant_index, ranks, tokens, split, cotangent, frozen_up_weight,
          tenant_down_adapters, tenant_up_adapters, jnp.asarray(eye, BF16))
        grad_up = grad_up.reshape(tenants // dp_n, rank, lf).astype(F32)
        grad_down = grad_down.reshape(tenants // dp_n, rank, ld).astype(F32)
        return (hidden, back, grad_down, grad_up)

    return shards


def solution(mesh):
    return jax.shard_map(
        make_shards(mesh),
        mesh=mesh,
        in_specs=(
            P(("fsdp", "dp"), "tenant"),
            P(("fsdp", "dp")),
            P(),
            P(("fsdp", "dp"), "tenant"),
            P("tenant", None, None),
            P("tenant", None, None),
            P(("fsdp", "dp"), "tenant"),
        ),
        out_specs=(
            P(("fsdp", "dp"), "tenant"),
            P(("fsdp", "dp"), "tenant"),
            P("dp", None, "tenant"),
            P("dp", None, "tenant"),
        ),
        check_vma=False,
    )
```

time: 265 us -> 225 us (0.85)
  Pallas kernels: 254 us -> 213 us
  local copies, waits for them, and re-layouts: 6.55 us -> 3.26 us
    pallas_call x1, Pallas kernels: 254 us -> 213 us  [shards(): pl.pallas_call(functools.partial(kernel, n, m), out_shape=(jax.ShapeDtype...]
    slice x2 -> x0, local copies, waits for them, and re-layouts: 3.46 us -> none  [the longest x1 2.32 us: shards(): grad_up = grads[:, :lf].reshape(tenants // dp_n, rank, lf)]
where the time goes in v1:
time: 225 us; the launch traced here: 221 us
  Pallas kernels  213 us (95%)
  other arithmetic  4.66 us (2%)
  local copies, waits for them, and re-layouts  3.26 us (1%)
    pallas_call x1, Pallas kernels, shards(): pl.pallas_call(functools.partial(kernel, n, m), out_shape=(jax.ShapeDtype...  213 us

profile of v1, /device:TPU:7, one launch (start us, length us, event | category | flops | bytes accessed | tf_op | source)
XLA Modules:
  0.0 221.1 jit_solution(325655717996686408)
XLA Ops:
  0.6 212.5 %shard_map.111 = (bf16[384,3584]{1,0:T(8,128)(2,1)}, bf16[384,1280]{1,0:T(8,128)(2,1)}, bf16[4,64,3584]{2,1,0:T(8,128)(2,1)}, bf16[4,64,1280]{2,1,0:T(8,128)(2,1)}, bf16[5,128,3584]{2,1,0:T(8,128)(2,1)}) custom-call(s32[6]{0:T(128)} %tenants_of.1, s32[8]{0:T(128)} %ranks.1, bf16[384,1280]{1,0:T(8,128)(2,1)} %split.1, bf16[384,1280]{1,0:T(8,128)(2,1)} %split.1, ...), custom_call_target="tpu_custom_call" | custom-call | tf_op jit(solution)/shard_map/pallas_call | solution.py:487
  213.2 0.0 copy-start.1
  213.2 2.4 %convert_element_type.6 = f32[4,64,1280]{2,1,0:T(8,128)} convert(bf16[4,64,1280]{2,1,0:T(8,128)(2,1)} %get-tuple-element.10) | non-fusion elementwise | flops 327680 | bytes 1966080 | tf_op jit(solution)/shard_map/convert_element_type | solution.py:537
  215.6 0.0 copy-done.1
  215.6 0.0 copy-start
  215.6 2.3 %convert_element_type.7 = f32[4,64,3584]{2,1,0:T(8,128)} convert(bf16[4,64,3584]{2,1,0:T(8,128)(2,1)S(1)} %copy-done.1) | non-fusion elementwise | flops 917504 | bytes 5505024 | tf_op jit(solution)/shard_map/convert_element_type | solution.py:536
  217.8 0.4 copy-done
  218.3 0.0 copy-start.2
  218.3 1.5 copy.14
  219.8 0.4 copy-done.2
  220.2 0.9 copy.15
Async XLA Ops:
  213.2 2.4 %copy-start.1 = (bf16[4,64,3584]{2,1,0:T(8,128)(2,1)S(1)}, bf16[4,64,3584]{2,1,0:T(8,128)(2,1)}, u32[]{:S(2)}) copy-start(bf16[4,64,3584]{2,1,0:T(8,128)(2,1)} %get-tuple-element.11) | copy-start | bytes 5505028
  215.6 2.7 %copy-start = (bf16[384,3584]{1,0:T(8,128)(2,1)S(1)}, bf16[384,3584]{1,0:T(8,128)(2,1)}, u32[]{:S(2)}) copy-start(bf16[384,3584]{1,0:T(8,128)(2,1)} %get-tuple-element.16) | copy-start | bytes 8257540
  218.3 1.9 copy-start.2

commit v2 on v1

--- a/solution.py
+++ b/solution.py
@@ -170,12 +170,16 @@
             part[s, cc, at] = (part[s, cc, at].astype(F32) + come[s, cc, at].astype(F32)).astype(BF16)
             hop(s, cc, h).start()
 
-    def combine_all(first, count, pos):
-        @pl.loop(0, 4 * count)
+    def combine_own(pos):
+        @pl.loop(0, 4)
         def _(i):
-            k = i // 4
-            s = first + k + (k // (half - 1)) * (1 if first else 0)
-            combine(s, (i // 2) % 2, i % 2, pos)
+            combine(0, i // 2, i % 2, pos)
+
+    def combine_near(cc, pos):
+        @pl.loop(0, 2 * (n - 2))
+        def _(i):
+            k = i // 2
+            combine(1 + k + k // (half - 1), cc, i % 2, pos)
 
     local[0].wait()
     local[1].wait()
@@ -262,6 +266,18 @@
     pass_tokens(1)
     for i in range(mid + 1, PIECES):
         relay(half - 2, i)
+
+    combine_own(1)
+    for i in range(n - 2):
+        s = 1 + i + i // (half - 1)
+        for q in range(PIECES):
+            rcopy(wbuf.at[1, phys(s), q], wbuf.at[1, phys(s), q], ds.at[s, q], dr.at[s, q], partner).wait_recv()
+
+    @pl.loop(0, 2 * (n - 2))
+    def _(i):
+        k = i % (n - 2)
+        product(1 + k + k // (half - 1), i // (n - 2), 1 + k)
+        first_hop(1 + k + k // (half - 1), i // (n - 2))
 
     for j in range(1, m):
         t = (z + j) % m
@@ -306,27 +322,13 @@
     grads(1 - c, None)
     swap = rcopy(gp, dpr, ps.at[0], pr.at[0], partner)
     swap.start()
-    combine_all(0, 1, 1)
+    for k in range(2, m - 1):
+        pass_tokens(k)
     swap.wait()
     grads(c, dpr)
-    for k in range(2, m - 1):
-        pass_tokens(k)
-
-    for i in range(n - 2):
-        s = 1 + i + i // (half - 1)
-        for q in range(PIECES):
-            rcopy(wbuf.at[1, phys(s), q], wbuf.at[1, phys(s), q], ds.at[s, q], dr.at[s, q], partner).wait_recv()
-
-    @pl.loop(0, 2 * (n - 2))
-    def _(i):
-        k = i // 2
-        product(1 + k + k // (half - 1), i % 2, 1 + k)
-        first_hop(1 + k + k // (half - 1), i % 2)
-
     for pos in range(2, m - 1):
-        combine_all(0, 1, pos)
-
-    pass_tokens(m - 1)
+        combine_own(pos)
+    combine_near(0, 1)
 
     def far(i):
         for way in range(2):
@@ -334,11 +336,7 @@
             arrived(half - 1, way, q, 0)
             across(half, q)
 
-    far(0)
-
     def forward(spots, body):
-        spots = [(s, cc, ph if isinstance(ph, tuple) else (cc, ph)) for s, cc, ph in spots]
-
         @pl.loop(0, lf // tile)
         def _(j):
             columns = pl.ds(pl.multiple_of(j * tile, tile), tile)
@@ -355,27 +353,60 @@
     def add_hid(columns, total):
         hid[:, columns] += total
 
-    for i in range(n - 2):
-        s = 1 + i + i // (half - 1)
-        forward(((s, 0, phys(s)), (s, 1, phys(s))), add_hid if i else set_hid)
-
-    for k in range(1, n):
-        peer = snake((place + k) % n, n)
-        start(rcopy(gp.at[pl.ds(pl.multiple_of(peer * quarter, 16), quarter)], rsr.at[k - 1], rs.at[k - 1],
-                    rr.at[k - 1], (peer, z, c)))
+    if n == 4:
+        d_first, d_last = owner(1), owner(n - 1)
+        later = ((d_first - z) * (d_first - z) > (d_last - z) * (d_last - z)).astype(jnp.int32)
+        turns = (later, 1 - later)
+    else:
+        pass_tokens(m - 1)
+        turns = range(n - 2)
+    for i, k in enumerate(turns):
+        s = 1 + k + k // (half - 1)
+        forward(((s, 0, (0, 1 + k)), (s, 1, (1, 1 + k))), add_hid if i else set_hid)
+        if n == 4 and i == 0:
+            pass_tokens(m - 1)
+            far(0)
+    if n != 4:
+        far(0)
+
+    across_dev = snake((place + half) % n, n)
+    hq = quarter // 2
+    strip = tile_of(lf + ld)
+    merged = n == 4
+
+    def rows_at(dev, h):
+        return pl.ds(pl.multiple_of(dev * quarter + h * hq, 16), hq)
+
+    def half_at(h):
+        return pl.ds(h * hq, hq)
+
+    def share_to(dev, h, slot, target):
+        return rcopy(gp.at[rows_at(dev, h)], rsr.at[slot, half_at(h)], rs.at[slot, h], rr.at[slot, h], target)
+
+    def share_from(slot, h):
+        there = rsr.at[slot, half_at(h)]
+        rcopy(there, there, rs.at[slot, h], rr.at[slot, h], partner).wait_recv()
+
+    if merged:
+        start(share_to(across_dev, 0, 0, to_right))
+        start(share_to(across_dev, 1, 0, to_left))
+        start(share_to(right, 1, 1, to_right))
+        start(share_to(left, 0, 2, to_left))
+    else:
+        for k in range(1, n):
+            peer = snake((place + k) % n, n)
+            for h in range(2):
+                start(share_to(peer, h, k - 1, (peer, z, c)))
 
     rcopy(pieces, pair_o, os.at[1], orr.at[1], partner).wait_recv()
     again = [pltpu.make_async_copy(pieces, wbuf.at[1, 1], l_sem.at[0]),
              pltpu.make_async_copy(pair_o, wbuf.at[1, 2], l_sem.at[1])]
     for copy in again:
         copy.start()
+    combine_near(1, 1)
+
     for i in range(1, mid):
         far(i)
-    combine_all(1, n - 2, 1)
-    for copy in again:
-        copy.wait()
-    forward(((0, 0, (1, 1)), (0, 1, (1, 2))), add_hid)
-
     arrived(half - 1, 0, mid, 0)
     across(half, mid)
     product(half, 0, 0)
@@ -384,8 +415,79 @@
         rcopy(wbuf.at[1, 0, q], wbuf.at[1, 0, q], ds.at[half, q], dr.at[half, q], partner).wait_recv()
     product(half, 1, 0)
     first_hop(half, 1)
+    if merged:
+        for h, dev, slot, target in ((0, right, 1, to_right), (1, left, 2, to_left)):
+            share_from(0, h)
+            at = rows_at(dev, h)
+
+            @pl.loop(0, (lf + ld) // strip)
+            def _(j):
+                columns = pl.ds(pl.multiple_of(j * strip, strip), strip)
+                total = gp[at, columns].astype(F32) + rsr[0, h * hq:(h + 1) * hq, columns].astype(F32)
+                gp[at, columns] = total.astype(BF16)
+
+            start(share_to(dev, h, slot, target))
     for pos in range(2, m - 1):
-        combine_all(1, n - 2, pos)
+        combine_near(0, pos)
+        combine_near(1, pos)
+
+    coming = sorted((2 * cc + h + 1.4 * pos, cc, h, pos) for cc in range(2) for h in range(2) for pos in range(1, m - 1))
+
+    def combine_next(count):
+        for _, cc, h, pos in coming[:count]:
+            combine(half, cc, h, pos)
+        del coming[:count]
+
+    combine_next(1)
+    for copy in again:
+        copy.wait()
+    forward(((0, 0, (1, 1)), (0, 1, (1, 2))), add_hid)
+    combine_next(1)
+
+    slots = range(1 if merged else 0, n - 1)
+    for slot in slots:
+        for h in range(2):
+            share_from(slot, h)
+
+    @pl.loop(0, (lf + ld) // strip)
+    def _(j):
+        columns = pl.ds(pl.multiple_of(j * strip, strip), strip)
+        total = gp[pl.ds(pl.multiple_of(f * quarter, 16), quarter), columns].astype(F32)
+        for slot in slots:
+            total = total + rsr[slot, :, columns].astype(F32)
+        ags[:, columns] = total.astype(BF16)
+
+    pair = ((slice(0, lf), gu_o), (slice(lf, lf + ld), gd_o))
+    keep = [pltpu.make_async_copy(ags.at[:, lanes], dst.at[f], o_sem.at[i]) for i, (lanes, dst) in enumerate(pair)]
+
+    def result_to(dev, h, slot, target, own_rows):
+        for i, (lanes, dst) in enumerate(pair):
+            there = dst.at[dev, half_at(h)]
+            start(rcopy(ags.at[half_at(h), lanes] if own_rows else there, there, qs.at[slot, h, i], qr.at[slot, h, i],
+                        target))
+
+    def result_from(dev, h, slot):
+        for i, (_, dst) in enumerate(pair):
+            there = dst.at[dev, half_at(h)]
+            rcopy(there, there, qs.at[slot, h, i], qr.at[slot, h, i], partner).wait_recv()
+
+    if merged:
+        for first in range(2):
+            result_to(f, first, 0, to_right, True)
+            result_to(f, 1 - first, 1, to_left, True)
+    else:
+        for k in range(1, n):
+            for h in range(2):
+                result_to(f, h, k - 1, (snake((place + k) % n, n), z, c), True)
+    for copy in keep:
+        copy.start()
+    combine_next(4)
+    if merged:
+        result_from(left, 0, 0)
+        result_to(left, 0, 2, to_right, False)
+        result_from(right, 1, 1)
+        result_to(right, 1, 2, to_left, False)
+    combine_next(len(coming))
 
     up_flat = tenants * rank
 
@@ -393,31 +495,9 @@
         total = total + nn(ada[...], upv[:, :, columns].reshape(up_flat, tile))
         cotv[:, columns] = (hid[:, columns] + total).astype(BF16)
 
-    forward(((half, 0, 0), (half, 1, 0)), finish)
+    forward(((half, 0, (0, 0)), (half, 1, (1, 0))), finish)
     hidden = pltpu.make_async_copy(cotv, hid_o, o_sem.at[2])
     hidden.start()
-    for h in range(2):
-        combine(half, 0, h, 1)
-
-    for k in range(1, n):
-        rcopy(rsr.at[k - 1], rsr.at[k - 1], rs.at[k - 1], rr.at[k - 1], partner).wait_recv()
-    total = gp[pl.ds(pl.multiple_of(f * quarter, 16), quarter), :].astype(F32)
-    for k in range(1, n):
-        total = total + rsr[k - 1].astype(F32)
-    ags[...] = total.astype(BF16)
-    pair = ((ags.at[:, :lf], gu_o), (ags.at[:, lf:], gd_o))
-    keep = [pltpu.make_async_copy(src, dst.at[f], o_sem.at[i]) for i, (src, dst) in enumerate(pair)]
-    for k in range(1, n):
-        for i, (src, dst) in enumerate(pair):
-            start(rcopy(src, dst.at[f], qs.at[k - 1, i], qr.at[k - 1, i], (snake((place + k) % n, n), z, c)))
-    for copy in keep:
-        copy.start()
-    for h in range(2):
-        combine(half, 1, h, 1)
-    for pos in range(2, m - 1):
-        for cc in range(2):
-            for h in range(2):
-                combine(half, cc, h, pos)
 
     s_z = (place + n - snake(z, n)) % n
     for slots, cond in (((n,), z == 0), ((s_z,), z == m - 1), ((s_z, n), (z > 0) & (z < m - 1))):
@@ -440,10 +520,13 @@
     back = pltpu.make_async_copy(tokv, gt_o, o_sem.at[3])
     back.start()
 
-    for k in range(1, n):
-        peer = snake((place + n - k) % n, n)
-        for i, (_, dst) in enumerate(pair):
-            rcopy(dst.at[peer], dst.at[peer], qs.at[k - 1, i], qr.at[k - 1, i], partner).wait_recv()
+    if merged:
+        for dev, h, slot in ((left, 1, 0), (right, 0, 1), (across_dev, 0, 2), (across_dev, 1, 2)):
+            result_from(dev, h, slot)
+    else:
+        for k in range(1, n):
+            for h in range(2):
+                result_from(snake((place + n - k) % n, n), h, k - 1)
     for cond, copy in sent:
         if cond is None:
             copy.wait_send()
@@ -523,8 +606,8 @@
                 dma((m - 1,)), dma((m,)),
                 dma((n, 2, 2)), dma((n + 1, 2, 2)),
                 dma((1,)), dma((1,)),
-                dma((n - 1,)), dma((n - 1,)),
                 dma((n - 1, 2)), dma((n - 1, 2)),
+                dma((n - 1, 2, 2)), dma((n - 1, 2, 2)),
                 dma((4,)),
                 pltpu.SemaphoreType.REGULAR((3,)),
             ],

time: 225 us -> 211 us (0.938); the launches traced: 221 us -> 211 us
  Pallas kernels: 213 us -> 202 us
    pallas_call x1, Pallas kernels: 213 us -> 202 us  [shards(): pl.pallas_call(functools.partial(kernel, n, m), out_shape=(jax.ShapeDtype...]
where the time goes in v2:
time: 211 us
  Pallas kernels  202 us (96%)
  other arithmetic  4.66 us (2%)
  local copies, waits for them, and re-layouts  3.26 us (2%)
    pallas_call x1, Pallas kernels, shards(): pl.pallas_call(functools.partial(kernel, n, m), out_shape=(jax.ShapeDtype...  202 us

profile of v2, /device:TPU:7, one launch (start us, length us, event | category | flops | bytes accessed | tf_op | source)
XLA Modules:
  0.0 210.6 jit_solution(10104491815518682259)
XLA Ops:
  0.6 202.1 %shard_map.111 = (bf16[384,3584]{1,0:T(8,128)(2,1)}, bf16[384,1280]{1,0:T(8,128)(2,1)}, bf16[4,64,3584]{2,1,0:T(8,128)(2,1)}, bf16[4,64,1280]{2,1,0:T(8,128)(2,1)}, bf16[5,128,3584]{2,1,0:T(8,128)(2,1)}) custom-call(s32[6]{0:T(128)} %tenants_of.1, s32[8]{0:T(128)} %ranks.1, bf16[384,1280]{1,0:T(8,128)(2,1)} %split.1, bf16[384,1280]{1,0:T(8,128)(2,1)} %split.1, ...), custom_call_target="tpu_custom_call" | custom-call | tf_op jit(solution)/shard_map/pallas_call | solution.py:570
  202.7 0.0 copy-start.1
  202.7 2.4 %convert_element_type.6 = f32[4,64,1280]{2,1,0:T(8,128)} convert(bf16[4,64,1280]{2,1,0:T(8,128)(2,1)} %get-tuple-element.10) | non-fusion elementwise | flops 327680 | bytes 1966080 | tf_op jit(solution)/shard_map/convert_element_type | solution.py:620
  205.1 0.0 copy-done.1
  205.1 0.0 copy-start
  205.1 2.3 %convert_element_type.7 = f32[4,64,3584]{2,1,0:T(8,128)} convert(bf16[4,64,3584]{2,1,0:T(8,128)(2,1)S(1)} %copy-done.1) | non-fusion elementwise | flops 917504 | bytes 5505024 | tf_op jit(solution)/shard_map/convert_element_type | solution.py:619
  207.4 0.4 copy-done
  207.8 0.0 copy-start.2
  207.8 1.5 copy.14
  209.3 0.4 copy-done.2
  209.7 0.9 copy.15
Async XLA Ops:
  202.7 2.4 %copy-start.1 = (bf16[4,64,3584]{2,1,0:T(8,128)(2,1)S(1)}, bf16[4,64,3584]{2,1,0:T(8,128)(2,1)}, u32[]{:S(2)}) copy-start(bf16[4,64,3584]{2,1,0:T(8,128)(2,1)} %get-tuple-element.11) | copy-start | bytes 5505028
  205.1 2.7 %copy-start = (bf16[384,3584]{1,0:T(8,128)(2,1)S(1)}, bf16[384,3584]{1,0:T(8,128)(2,1)}, u32[]{:S(2)}) copy-start(bf16[384,3584]{1,0:T(8,128)(2,1)} %get-tuple-element.16) | copy-start | bytes 8257540
  207.8 1.9 copy-start.2

commit v3 on v2

--- a/solution.py
+++ b/solution.py
@@ -42,6 +42,34 @@
     row, col = i // side, i % side
     odd = row % 2
     return row * side + (1 - odd) * col + odd * (side - 1 - col)
+
+
+def finish_kernel(hid_i, gt_i, gu_i, gd_i, hid_o, gt_o, gu_o, gd_o, hv, tv, uv, dv, uf, df, i_sem, o_sem):
+    n = gu_i.shape[0]
+    quarter = gu_i.shape[1]
+    fetch = [pltpu.make_async_copy(gu_i.at[k], uv.at[k], i_sem.at[k]) for k in range(n)]
+    fetch += [pltpu.make_async_copy(gd_i, dv, i_sem.at[n]), pltpu.make_async_copy(hid_i, hv, i_sem.at[n + 1]),
+              pltpu.make_async_copy(gt_i, tv, i_sem.at[n + 2])]
+    for copy in fetch:
+        copy.start()
+    put = []
+    for k in range(n):
+        fetch[k].wait()
+        for r in range(quarter // 16):
+            uf[k, r * 16:(r + 1) * 16] = uv[k, r * 16:(r + 1) * 16].astype(F32)
+        put.append(pltpu.make_async_copy(uf.at[k], gu_o.at[k], o_sem.at[k]))
+        put[-1].start()
+    fetch[n].wait()
+    for k in range(n):
+        df[k] = dv[k].astype(F32)
+    put.append(pltpu.make_async_copy(df, gd_o, o_sem.at[n]))
+    put[-1].start()
+    for i, (src, dst) in enumerate(((hv, hid_o), (tv, gt_o))):
+        fetch[n + 1 + i].wait()
+        put.append(pltpu.make_async_copy(src, dst, o_sem.at[n + 1 + i]))
+        put[-1].start()
+    for copy in put:
+        copy.wait()
 
 
 def kernel(n, m, tenants_of, ranks, tokens, split, cot, w, dn, up, eye,
@@ -336,8 +364,8 @@
             arrived(half - 1, way, q, 0)
             across(half, q)
 
-    def forward(spots, body):
-        @pl.loop(0, lf // tile)
+    def forward(spots, body, first=0, last=lf // tile):
+        @pl.loop(first, last)
         def _(j):
             columns = pl.ds(pl.multiple_of(j * tile, tile), tile)
             total = None
@@ -371,7 +399,6 @@
 
     across_dev = snake((place + half) % n, n)
     hq = quarter // 2
-    strip = tile_of(lf + ld)
     merged = n == 4
 
     def rows_at(dev, h):
@@ -380,23 +407,28 @@
     def half_at(h):
         return pl.ds(h * hq, hq)
 
-    def share_to(dev, h, slot, target):
-        return rcopy(gp.at[rows_at(dev, h)], rsr.at[slot, half_at(h)], rs.at[slot, h], rr.at[slot, h], target)
-
-    def share_from(slot, h):
-        there = rsr.at[slot, half_at(h)]
-        rcopy(there, there, rs.at[slot, h], rr.at[slot, h], partner).wait_recv()
-
-    if merged:
-        start(share_to(across_dev, 0, 0, to_right))
-        start(share_to(across_dev, 1, 0, to_left))
-        start(share_to(right, 1, 1, to_right))
-        start(share_to(left, 0, 2, to_left))
-    else:
-        for k in range(1, n):
-            peer = snake((place + k) % n, n)
-            for h in range(2):
-                start(share_to(peer, h, k - 1, (peer, z, c)))
+    parts = ((slice(0, lf), gu_o), (slice(lf, lf + ld), gd_o))
+
+    def share_to(i, dev, h, slot, target):
+        lanes = parts[i][0]
+        return rcopy(gp.at[rows_at(dev, h), lanes], rsr.at[slot, half_at(h), lanes], rs.at[slot, h, i],
+                     rr.at[slot, h, i], target)
+
+    def share_from(i, slot, h):
+        there = rsr.at[slot, half_at(h), parts[i][0]]
+        rcopy(there, there, rs.at[slot, h, i], rr.at[slot, h, i], partner).wait_recv()
+
+    for i in range(2):
+        if merged:
+            start(share_to(i, across_dev, 0, 0, to_right))
+            start(share_to(i, across_dev, 1, 0, to_left))
+            start(share_to(i, right, 1, 1, to_right))
+            start(share_to(i, left, 0, 2, to_left))
+        else:
+            for k in range(1, n):
+                peer = snake((place + k) % n, n)
+                for h in range(2):
+                    start(share_to(i, peer, h, k - 1, (peer, z, c)))
 
     rcopy(pieces, pair_o, os.at[1], orr.at[1], partner).wait_recv()
     again = [pltpu.make_async_copy(pieces, wbuf.at[1, 1], l_sem.at[0]),
@@ -415,18 +447,28 @@
         rcopy(wbuf.at[1, 0, q], wbuf.at[1, 0, q], ds.at[half, q], dr.at[half, q], partner).wait_recv()
     product(half, 1, 0)
     first_hop(half, 1)
-    if merged:
+    def strips(i, body):
+        lanes = parts[i][0]
+        strip = tile_of(lanes.stop - lanes.start, 256)
+
+        @pl.loop(0, (lanes.stop - lanes.start) // strip)
+        def _(j):
+            body(pl.ds(pl.multiple_of(lanes.start + j * strip, 128), strip))
+
+    def merge(i):
         for h, dev, slot, target in ((0, right, 1, to_right), (1, left, 2, to_left)):
-            share_from(0, h)
+            share_from(i, 0, h)
             at = rows_at(dev, h)
 
-            @pl.loop(0, (lf + ld) // strip)
-            def _(j):
-                columns = pl.ds(pl.multiple_of(j * strip, strip), strip)
+            def add(columns):
                 total = gp[at, columns].astype(F32) + rsr[0, h * hq:(h + 1) * hq, columns].astype(F32)
                 gp[at, columns] = total.astype(BF16)
 
-            start(share_to(dev, h, slot, target))
+            strips(i, add)
+            start(share_to(i, dev, h, slot, target))
+
+    if merged:
+        merge(0)
     for pos in range(2, m - 1):
         combine_near(0, pos)
         combine_near(1, pos)
@@ -439,63 +481,76 @@
         del coming[:count]
 
     combine_next(1)
+    if merged:
+        merge(1)
     for copy in again:
         copy.wait()
     forward(((0, 0, (1, 1)), (0, 1, (1, 2))), add_hid)
     combine_next(1)
 
     slots = range(1 if merged else 0, n - 1)
-    for slot in slots:
-        for h in range(2):
-            share_from(slot, h)
-
-    @pl.loop(0, (lf + ld) // strip)
-    def _(j):
-        columns = pl.ds(pl.multiple_of(j * strip, strip), strip)
-        total = gp[pl.ds(pl.multiple_of(f * quarter, 16), quarter), columns].astype(F32)
+    keep = []
+
+    def result_to(i, dev, h, slot, target, own_rows):
+        lanes, dst = parts[i]
+        there = dst.at[dev, half_at(h)]
+        start(rcopy(ags.at[half_at(h), lanes] if own_rows else there, there, qs.at[slot, h, i], qr.at[slot, h, i],
+                    target))
+
+    def result_from(i, dev, h, slot):
+        there = parts[i][1].at[dev, half_at(h)]
+        rcopy(there, there, qs.at[slot, h, i], qr.at[slot, h, i], partner).wait_recv()
+
+    def result(i):
         for slot in slots:
-            total = total + rsr[slot, :, columns].astype(F32)
-        ags[:, columns] = total.astype(BF16)
-
-    pair = ((slice(0, lf), gu_o), (slice(lf, lf + ld), gd_o))
-    keep = [pltpu.make_async_copy(ags.at[:, lanes], dst.at[f], o_sem.at[i]) for i, (lanes, dst) in enumerate(pair)]
-
-    def result_to(dev, h, slot, target, own_rows):
-        for i, (lanes, dst) in enumerate(pair):
-            there = dst.at[dev, half_at(h)]
-            start(rcopy(ags.at[half_at(h), lanes] if own_rows else there, there, qs.at[slot, h, i], qr.at[slot, h, i],
-                        target))
-
-    def result_from(dev, h, slot):
-        for i, (_, dst) in enumerate(pair):
-            there = dst.at[dev, half_at(h)]
-            rcopy(there, there, qs.at[slot, h, i], qr.at[slot, h, i], partner).wait_recv()
-
-    if merged:
-        for first in range(2):
-            result_to(f, first, 0, to_right, True)
-            result_to(f, 1 - first, 1, to_left, True)
-    else:
-        for k in range(1, n):
             for h in range(2):
-                result_to(f, h, k - 1, (snake((place + k) % n, n), z, c), True)
-    for copy in keep:
-        copy.start()
-    combine_next(4)
-    if merged:
-        result_from(left, 0, 0)
-        result_to(left, 0, 2, to_right, False)
-        result_from(right, 1, 1)
-        result_to(right, 1, 2, to_left, False)
-    combine_next(len(coming))
+                share_from(i, slot, h)
+
+        def add(columns):
+            total = gp[pl.ds(pl.multiple_of(f * quarter, 16), quarter), columns].astype(F32)
+            for slot in slots:
+                total = total + rsr[slot, :, columns].astype(F32)
+            ags[:, columns] = total.astype(BF16)
+
+        strips(i, add)
+        if merged:
+            for first in range(2):
+                result_to(i, f, first, 0, to_right, True)
+                result_to(i, f, 1 - first, 1, to_left, True)
+        else:
+            for k in range(1, n):
+                for h in range(2):
+                    result_to(i, f, h, k - 1, (snake((place + k) % n, n), z, c), True)
+        lanes, dst = parts[i]
+        keep.append(pltpu.make_async_copy(ags.at[:, lanes], dst.at[f], o_sem.at[i]))
+        keep[-1].start()
+
+    def result_on(i):
+        if merged:
+            result_from(i, left, 0, 0)
+            result_to(i, left, 0, 2, to_right, False)
+            result_from(i, right, 1, 1)
+            result_to(i, right, 1, 2, to_left, False)
+
+    result(0)
+    combine_next(1)
+    result(1)
+    combine_next(3)
+    result_on(0)
 
     up_flat = tenants * rank
+    farthest = ((half, 0, (0, 0)), (half, 1, (1, 0)))
+    early = lf // tile // 2
 
     def finish(columns, total):
         total = total + nn(ada[...], upv[:, :, columns].reshape(up_flat, tile))
         cotv[:, columns] = (hid[:, columns] + total).astype(BF16)
 
-    forward(((half, 0, (0, 0)), (half, 1, (1, 0))), finish)
+    forward(farthest, finish, 0, early)
+    combine_next(len(coming))
+    result_on(1)
+
+    forward(farthest, finish, early)
     hidden = pltpu.make_async_copy(cotv, hid_o, o_sem.at[2])
     hidden.start()
 
@@ -520,13 +575,14 @@
     back = pltpu.make_async_copy(tokv, gt_o, o_sem.at[3])
     back.start()
 
-    if merged:
-        for dev, h, slot in ((left, 1, 0), (right, 0, 1), (across_dev, 0, 2), (across_dev, 1, 2)):
-            result_from(dev, h, slot)
-    else:
-        for k in range(1, n):
-            for h in range(2):
-                result_from(snake((place + n - k) % n, n), h, k - 1)
+    for i in range(2):
+        if merged:
+            for dev, h, slot in ((left, 1, 0), (right, 0, 1), (across_dev, 0, 2), (across_dev, 1, 2)):
+                result_from(i, dev, h, slot)
+        else:
+            for k in range(1, n):
+                for h in range(2):
+                    result_from(i, snake((place + n - k) % n, n), h, k - 1)
     for cond, copy in sent:
         if cond is None:
             copy.wait_send()
@@ -606,7 +662,7 @@
                 dma((m - 1,)), dma((m,)),
                 dma((n, 2, 2)), dma((n + 1, 2, 2)),
                 dma((1,)), dma((1,)),
-                dma((n - 1, 2)), dma((n - 1, 2)),
+                dma((n - 1, 2, 2)), dma((n - 1, 2, 2)),
                 dma((n - 1, 2, 2)), dma((n - 1, 2, 2)),
                 dma((4,)),
                 pltpu.SemaphoreType.REGULAR((3,)),
@@ -616,8 +672,21 @@
             ),
         )(block_tenant_index, ranks, tokens, split, cotangent, frozen_up_weight,
           tenant_down_adapters, tenant_up_adapters, jnp.asarray(eye, BF16))
-        grad_up = grad_up.reshape(tenants // dp_n, rank, lf).astype(F32)
-        grad_down = grad_down.reshape(tenants // dp_n, rank, ld).astype(F32)
+        results = (hidden, back, grad_up, grad_down)
+        hidden, back, grad_up, grad_down = pl.pallas_call(
+            finish_kernel,
+            out_shape=tuple(
+                jax.ShapeDtypeStruct(x.shape, F32 if x.ndim == 3 else BF16) for x in results
+            ),
+            in_specs=[any_space] * 4,
+            out_specs=(any_space,) * 4,
+            scratch_shapes=[pltpu.VMEM(x.shape, BF16) for x in results]
+            + [pltpu.VMEM(x.shape, F32) for x in results[2:]]
+            + [dma((n + 3,)), dma((n + 3,))],
+            compiler_params=pltpu.CompilerParams(vmem_limit_bytes=67043328),
+        )(*results)
+        grad_up = grad_up.reshape(tenants // dp_n, rank, lf)
+        grad_down = grad_down.reshape(tenants // dp_n, rank, ld)
         return (hidden, back, grad_down, grad_up)
 
     return shards

time: 211 us -> 208 us (0.986)
  Pallas kernels: 202 us -> 207 us
  other arithmetic: 4.66 us -> 0 us
  local copies, waits for them, and re-layouts: 3.26 us -> 0 us
    pallas_call x0 -> x1, Pallas kernels: none -> 5.71 us  [shards(): pl.pallas_call(finish_kernel, out_shape=tuple((jax.ShapeDtypeStruct(x.sha...]
    convert_element_type x2 -> x0, other arithmetic: 4.66 us -> none  [the longest x1 2.38 us: shards(): grad_down = grad_down.reshape(tenants // dp_n, rank, ld).astype(F32)]
    unnamed x8 -> x0, local copies, waits for them, and re-layouts: 3.26 us -> none
where the time goes in v3:
time: 208 us
  Pallas kernels  207 us (100%)
    pallas_call x1, Pallas kernels, shards(): pl.pallas_call(functools.partial(kernel, n, m), out_shape=(jax.ShapeDtype...  202 us
    pallas_call x1, Pallas kernels, shards(): pl.pallas_call(finish_kernel, out_shape=tuple((jax.ShapeDtypeStruct(x.sha...  5.71 us

profile of v3, /device:TPU:7, one launch (start us, length us, event | category | flops | bytes accessed | tf_op | source)
XLA Modules:
  0.0 208.3 jit_solution(8129797837840444512)
XLA Ops:
  0.6 201.8 %shard_map.111 = (bf16[384,3584]{1,0:T(8,128)(2,1)}, bf16[384,1280]{1,0:T(8,128)(2,1)}, bf16[4,64,3584]{2,1,0:T(8,128)(2,1)}, bf16[4,64,1280]{2,1,0:T(8,128)(2,1)}, bf16[5,128,3584]{2,1,0:T(8,128)(2,1)}) custom-call(s32[6]{0:T(128)} %tenants_of.1, s32[8]{0:T(128)} %ranks.1, bf16[384,1280]{1,0:T(8,128)(2,1)} %split.1, bf16[384,1280]{1,0:T(8,128)(2,1)} %split.1, ...), custom_call_target="tpu_custom_call" | custom-call | tf_op jit(solution)/shard_map/pallas_call | solution.py:626
  202.4 5.7 %shard_map.112 = (bf16[384,3584]{1,0:T(8,128)(2,1)}, bf16[384,1280]{1,0:T(8,128)(2,1)}, f32[4,64,3584]{2,1,0:T(8,128)}, f32[4,64,1280]{2,1,0:T(8,128)}) custom-call(bf16[384,3584]{1,0:T(8,128)(2,1)} %get-tuple-element.12.hid_i, bf16[384,1280]{1,0:T(8,128)(2,1)} %get-tuple-element.13.gt_i, bf16[4,64,3584]{2,1,0:T(8,128)(2,1)} %get-tuple-element.14.gu_i, ...), custom_call_target="tpu_custom_call" | custom-call | tf_op jit(solution)/shard_map/pallas_call | solution.py:676

commit v4 on v3

--- a/solution.py
+++ b/solution.py
@@ -11,6 +11,7 @@
 
 BLOCK = 64
 PIECES = 5
+BANDS = 4
 
 alpha_scale = 32.0
 
@@ -165,7 +166,7 @@
         start(rcopy(tok_src(ca), tv.at[z, ca], ts.at[0, 1, ca], tr.at[z, ca], plane(z - 1)), z > 0)
 
     def rows_of(h):
-        return pl.ds(pl.multiple_of(h * (rows // 2), 16), rows // 2)
+        return pl.ds(pl.multiple_of(h * (rows // BANDS), 16), rows // BANDS)
 
     def hop(s, cc, h):
         d = owner(s)
@@ -185,7 +186,7 @@
 
         @pl.when(((d > z) & (z == 0)) | ((d < z) & (z == m - 1)))
         def _():
-            for h in range(2):
+            for h in range(BANDS):
                 hop(s, cc, h).start()
 
     def combine(s, cc, h, pos):
@@ -199,15 +200,15 @@
             hop(s, cc, h).start()
 
     def combine_own(pos):
-        @pl.loop(0, 4)
+        @pl.loop(0, 2 * BANDS)
         def _(i):
-            combine(0, i // 2, i % 2, pos)
+            combine(0, i // BANDS, i % BANDS, pos)
 
     def combine_near(cc, pos):
-        @pl.loop(0, 2 * (n - 2))
+        @pl.loop(0, BANDS * (n - 2))
         def _(i):
-            k = i // 2
-            combine(1 + k + k // (half - 1), cc, i % 2, pos)
+            k = i // BANDS
+            combine(1 + k + k // (half - 1), cc, i % BANDS, pos)
 
     local[0].wait()
     local[1].wait()
@@ -473,20 +474,21 @@
         combine_near(0, pos)
         combine_near(1, pos)
 
-    coming = sorted((2 * cc + h + 1.4 * pos, cc, h, pos) for cc in range(2) for h in range(2) for pos in range(1, m - 1))
+    coming = sorted(
+        (BANDS * cc + h + 2 * pos, pos, cc, h) for cc in range(2) for h in range(BANDS) for pos in range(1, m - 1))
 
     def combine_next(count):
-        for _, cc, h, pos in coming[:count]:
+        for _, pos, cc, h in coming[:count]:
             combine(half, cc, h, pos)
         del coming[:count]
 
-    combine_next(1)
+    combine_next(2)
     if merged:
         merge(1)
     for copy in again:
         copy.wait()
     forward(((0, 0, (1, 1)), (0, 1, (1, 2))), add_hid)
-    combine_next(1)
+    combine_next(4)
 
     slots = range(1 if merged else 0, n - 1)
     keep = []
@@ -533,9 +535,8 @@
             result_to(i, right, 1, 2, to_left, False)
 
     result(0)
-    combine_next(1)
     result(1)
-    combine_next(3)
+    combine_next(6)
     result_on(0)
 
     up_flat = tenants * rank
@@ -546,6 +547,7 @@
         total = total + nn(ada[...], upv[:, :, columns].reshape(up_flat, tile))
         cotv[:, columns] = (hid[:, columns] + total).astype(BF16)
 
+    combine_next(2)
     forward(farthest, finish, 0, early)
     combine_next(len(coming))
     result_on(1)
@@ -560,7 +562,7 @@
         def _():
             for slot in slots:
                 for cc in range(2):
-                    for h in range(2):
+                    for h in range(BANDS):
                         at = rows_of(h)
                         rcopy(come.at[slot, cc, at], come.at[slot, cc, at], gs.at[0, cc, h], gr.at[slot, cc, h],
                               partner).wait_recv()
@@ -590,7 +592,7 @@
             pl.when(cond)(copy.wait_send)
     for s in range(n):
         for cc in range(2):
-            for h in range(2):
+            for h in range(BANDS):
                 pl.when(owner(s) != z)(hop(s, cc, h).wait_send)
     for copy in keep:
         copy.wait()
@@ -660,7 +662,7 @@
                 dma((2, m - 1, 2)), dma((2, m - 1, 2)),
                 dma((2, m - 1, 2)), dma((2, m - 1, 2)),
                 dma((m - 1,)), dma((m,)),
-                dma((n, 2, 2)), dma((n + 1, 2, 2)),
+                dma((n, 2, BANDS)), dma((n + 1, 2, BANDS)),
                 dma((1,)), dma((1,)),
                 dma((n - 1, 2, 2)), dma((n - 1, 2, 2)),
                 dma((n - 1, 2, 2)), dma((n - 1, 2, 2)),

time: 208 us -> 207 us (level)
  no operation moved by 1% of the time
where the time goes in v4:
time: 207 us; the launch traced here: 206 us
  Pallas kernels  206 us (100%)
    pallas_call x1, Pallas kernels, shards(): pl.pallas_call(functools.partial(kernel, n, m), out_shape=(jax.ShapeDtype...  200 us
    pallas_call x1, Pallas kernels, shards(): pl.pallas_call(finish_kernel, out_shape=tuple((jax.ShapeDtypeStruct(x.sha...  5.71 us

profile of v4, /device:TPU:7, one launch (start us, length us, event | category | flops | bytes accessed | tf_op | source)
XLA Modules:
  0.0 206.4 jit_solution(7456770455486614030)
XLA Ops:
  0.6 199.9 %shard_map.111 = (bf16[384,3584]{1,0:T(8,128)(2,1)}, bf16[384,1280]{1,0:T(8,128)(2,1)}, bf16[4,64,3584]{2,1,0:T(8,128)(2,1)}, bf16[4,64,1280]{2,1,0:T(8,128)(2,1)}, bf16[5,128,3584]{2,1,0:T(8,128)(2,1)}) custom-call(s32[6]{0:T(128)} %tenants_of.1, s32[8]{0:T(128)} %ranks.1, bf16[384,1280]{1,0:T(8,128)(2,1)} %split.1, bf16[384,1280]{1,0:T(8,128)(2,1)} %split.1, ...), custom_call_target="tpu_custom_call" | custom-call | tf_op jit(solution)/shard_map/pallas_call | solution.py:628
  200.5 5.7 %shard_map.112 = (bf16[384,3584]{1,0:T(8,128)(2,1)}, bf16[384,1280]{1,0:T(8,128)(2,1)}, f32[4,64,3584]{2,1,0:T(8,128)}, f32[4,64,1280]{2,1,0:T(8,128)}) custom-call(bf16[384,3584]{1,0:T(8,128)(2,1)} %get-tuple-element.12.hid_i, bf16[384,1280]{1,0:T(8,128)(2,1)} %get-tuple-element.13.gt_i, bf16[4,64,3584]{2,1,0:T(8,128)(2,1)} %get-tuple-element.14.gu_i, ...), custom_call_target="tpu_custom_call" | custom-call | tf_op jit(solution)/shard_map/pallas_call | solution.py:678

commit v5 on v4

--- a/solution.py
+++ b/solution.py
@@ -48,34 +48,38 @@
 def finish_kernel(hid_i, gt_i, gu_i, gd_i, hid_o, gt_o, gu_o, gd_o, hv, tv, uv, dv, uf, df, i_sem, o_sem):
     n = gu_i.shape[0]
     quarter = gu_i.shape[1]
+    plain = [pltpu.make_async_copy(hid_i, hv, i_sem.at[n + 1]), pltpu.make_async_copy(gt_i, tv, i_sem.at[n + 2])]
     fetch = [pltpu.make_async_copy(gu_i.at[k], uv.at[k], i_sem.at[k]) for k in range(n)]
-    fetch += [pltpu.make_async_copy(gd_i, dv, i_sem.at[n]), pltpu.make_async_copy(hid_i, hv, i_sem.at[n + 1]),
-              pltpu.make_async_copy(gt_i, tv, i_sem.at[n + 2])]
-    for copy in fetch:
+    fetch.append(pltpu.make_async_copy(gd_i, dv, i_sem.at[n]))
+    for copy in fetch[:1] + plain[:1] + fetch[1:] + plain[1:]:
         copy.start()
     put = []
+
+    def out(src, dst, k):
+        put.append(pltpu.make_async_copy(src, dst, o_sem.at[k]))
+        put[-1].start()
+
     for k in range(n):
         fetch[k].wait()
         for r in range(quarter // 16):
             uf[k, r * 16:(r + 1) * 16] = uv[k, r * 16:(r + 1) * 16].astype(F32)
-        put.append(pltpu.make_async_copy(uf.at[k], gu_o.at[k], o_sem.at[k]))
-        put[-1].start()
+        out(uf.at[k], gu_o.at[k], k)
+        if k == 0:
+            plain[0].wait()
+            out(hv, hid_o, n + 1)
     fetch[n].wait()
     for k in range(n):
         df[k] = dv[k].astype(F32)
-    put.append(pltpu.make_async_copy(df, gd_o, o_sem.at[n]))
-    put[-1].start()
-    for i, (src, dst) in enumerate(((hv, hid_o), (tv, gt_o))):
-        fetch[n + 1 + i].wait()
-        put.append(pltpu.make_async_copy(src, dst, o_sem.at[n + 1 + i]))
-        put[-1].start()
+    out(df, gd_o, n)
+    plain[1].wait()
+    out(tv, gt_o, n + 2)
     for copy in put:
         copy.wait()
 
 
-def kernel(n, m, tenants_of, ranks, tokens, split, cot, w, dn, up, eye,
+def kernel(n, m, tenants_of, ranks, tokens, split, cot, w, dn, up, eye_i,
            hid_o, gt_o, gu_o, gd_o, pair_o,
-           wbuf, cotv, tokv, tv, hid, upv, dnv, part, come, gp, dpr, rsr, ags, sums, ada, adg,
+           wbuf, cotv, tokv, tv, hid, upv, dnv, part, come, gp, dpr, rsr, ags, sums, ada, adg, eye,
            l_sem, ws, wr, os, orr, ds, dr, ts, tr, as_, ar, xs, xr, ss, sr, gs, gr, ps, pr, rs, rr, qs, qr, o_sem, cred):
     f, z, c = lax.axis_index("fsdp"), lax.axis_index("tenant"), lax.axis_index("dp")
     rows, ld = tokens.shape
@@ -138,6 +142,7 @@
             dn.at[:, :, pl.ds(pl.multiple_of(z * ld, 128), ld)], dnv.at[pl.ds(z * own, own)], l_sem.at[5]),
         pltpu.make_async_copy(
             up.at[:, :, pl.ds(pl.multiple_of(z * lf, 128), lf)], upv.at[pl.ds(z * own, own)], l_sem.at[6]),
+        pltpu.make_async_copy(eye_i, eye, l_sem.at[7]),
     ]
     for copy in local:
         copy.start()
@@ -634,8 +639,7 @@
                 jax.ShapeDtypeStruct((n, quarter, ld), BF16),
                 jax.ShapeDtypeStruct((PIECES, piece, lf), BF16),
             ),
-            in_specs=[pl.BlockSpec(memory_space=pltpu.SMEM)] * 2 + [any_space] * 6
-            + [pl.BlockSpec(memory_space=pltpu.VMEM)],
+            in_specs=[pl.BlockSpec(memory_space=pltpu.SMEM)] * 2 + [any_space] * 7,
             out_specs=(any_space,) * 5,
             scratch_shapes=[
                 pltpu.VMEM((2, n - 1, PIECES, piece, lf), BF16),
@@ -654,7 +658,8 @@
                 pltpu.VMEM((m, rows, 2 * rank), F32),
                 pltpu.VMEM((rows, tenants * rank), BF16),
                 pltpu.VMEM((rows, tenants * rank), BF16),
-                dma((7,)),
+                pltpu.VMEM(eye.shape, BF16),
+                dma((8,)),
                 dma((half, 2, PIECES)), dma((half, 2, PIECES)),
                 dma((2,)), dma((2,)),
                 dma((n, PIECES)), dma((n, PIECES)),

time: 207 us -> 206 us (level)
  no operation moved by 1% of the time
where the time goes in v5:
time: 206 us
  Pallas kernels  205 us (100%)
    pallas_call x1, Pallas kernels, shards(): pl.pallas_call(functools.partial(kernel, n, m), out_shape=(jax.ShapeDtype...  200 us
    pallas_call x1, Pallas kernels, shards(): pl.pallas_call(finish_kernel, out_shape=tuple((jax.ShapeDtypeStruct(x.sha...  5.15 us

profile of v5, /device:TPU:7, one launch (start us, length us, event | category | flops | bytes accessed | tf_op | source)
XLA Modules:
  0.0 205.5 jit_solution(18324619371276072214)
XLA Ops:
  0.6 199.6 %shard_map.111 = (bf16[384,3584]{1,0:T(8,128)(2,1)}, bf16[384,1280]{1,0:T(8,128)(2,1)}, bf16[4,64,3584]{2,1,0:T(8,128)(2,1)}, bf16[4,64,1280]{2,1,0:T(8,128)(2,1)}, bf16[5,128,3584]{2,1,0:T(8,128)(2,1)}) custom-call(s32[6]{0:T(128)} %tenants_of.1, s32[8]{0:T(128)} %ranks.1, bf16[384,1280]{1,0:T(8,128)(2,1)} %split.1, bf16[384,1280]{1,0:T(8,128)(2,1)} %split.1, ...), custom_call_target="tpu_custom_call" | custom-call | tf_op jit(solution)/shard_map/pallas_call | solution.py:633
  200.2 5.2 %shard_map.112 = (bf16[384,3584]{1,0:T(8,128)(2,1)}, bf16[384,1280]{1,0:T(8,128)(2,1)}, f32[4,64,3584]{2,1,0:T(8,128)}, f32[4,64,1280]{2,1,0:T(8,128)}) custom-call(bf16[384,3584]{1,0:T(8,128)(2,1)} %get-tuple-element.12.hid_i, bf16[384,1280]{1,0:T(8,128)(2,1)} %get-tuple-element.13.gt_i, bf16[4,64,3584]{2,1,0:T(8,128)(2,1)} %get-tuple-element.14.gu_i, ...), custom_call_target="tpu_custom_call" | custom-call | tf_op jit(solution)/shard_map/pallas_call | solution.py:683
